TPU v7x, 128 devices: a whole 4x4x4 slice. The times are simulated.
128 devices in a mesh: batch: 8 (over z, core), seq: 16 (over x, y).
Axes of the slice: x: 4, y: 4, z: 4, core: 2. Of those that a mesh axis runs over, the one named last changes fastest.
Arguments:
- queries: bfloat16 [65536, 8, 256], P(('batch', 'seq')), parts along dimension 0, may hold values from -400 to 400
- key_heads: bfloat16 [65536, 4, 256], P(('batch', 'seq')), parts along dimension 0, may hold values from -16 to 16
- projected_value_heads: bfloat16 [65536, 4, 256], P(('batch', 'seq')), parts along dimension 0, may hold values from -6 to 6
- lengths: int32 [8], P('batch'), parts along dimension 0, may hold values from 7681 to 8192
Outputs:
- attended: bfloat16 [65536, 8, 256], P(('batch', 'seq')), parts along dimension 0
There are 8 independent parts, one for each index of `batch`. A program takes and returns all parts, laid end to end along the dimension named above; each array names one. Nothing has to cross between parts.
All inputs are finite; a program needn't handle non-finite values.
Results may differ from a plain program's by a relative error of at most 0.0033.
Values may be sent and summed in bfloat16 or wider, within the bound.
A program may use at most 192 MiB of HBM per device.

v0:
```python
import math
import jax
import jax.numpy as jnp
from jax import lax
from jax.sharding import PartitionSpec as P

WINDOW = 4096
SINKS = 4


def broadcast(x, axis, root):
    return lax.dynamic_index_in_dim(lax.all_gather(x, axis), root, 0, keepdims=False)


def shards(queries, key_heads, projected_value_heads, lengths):
    tok_rows = queries.shape[0]
    head_count = queries.shape[1]
    head_width = queries.shape[2]
    kv_heads = key_heads.shape[1]
    share = head_count // kv_heads
    position = lax.axis_index("seq")
    length_now = lengths[0]
    first_row = position * tok_rows
    score_scale = head_width ** (-0.5)
    grouped = queries.reshape(tok_rows, kv_heads, share, head_width)
    query_pos = first_row + jnp.arange(tok_rows, dtype=jnp.int32)
    last_query = first_row + tok_rows - 1

    def attend(running, kv_block, key_start, sink_mode):
        key_count = kv_block.shape[1]
        key_pos = key_start + jnp.arange(key_count, dtype=jnp.int32)
        if sink_mode:
            useful = first_row < length_now
        else:
            useful = (
                (key_start <= last_query)
                & (key_start + key_count - 1 > first_row - WINDOW)
                & (key_start < length_now)
                & (first_row < length_now)
                & (key_start + key_count > SINKS)
            )

        def compute(current):
            maximum, totals, weighted = current
            scores = (
                jnp.einsum(
                    "qhgd,khd->hgqk", grouped, kv_block[0], preferred_element_type=jnp.float32
                )
                * score_scale
            )
            distance = query_pos[:, None] - key_pos[None, :]
            if sink_mode:
                visible = (distance >= 0) & (key_pos[None, :] < length_now)
            else:
                visible = (
                    (distance >= 0)
                    & (distance < WINDOW)
                    & (key_pos[None, :] >= SINKS)
                    & (key_pos[None, :] < length_now)
                )
            visible = visible & (query_pos[:, None] < length_now)
            masked = jnp.where(visible, scores, -1e30)
            newest = jnp.maximum(maximum, jnp.max(masked, axis=-1))
            weights = jnp.where(visible, jnp.exp(scores - newest[..., None]), 0.0)
            rescale = jnp.exp(maximum - newest)
            totals = totals * rescale + jnp.sum(weights, axis=-1)
            weighted = weighted * rescale[..., None] + jnp.einsum(
                "hgqk,khd->hgqd",
                weights.astype(jnp.bfloat16),
                kv_block[1],
                preferred_element_type=jnp.float32,
            )
            return (newest, totals, weighted)

        return lax.cond(useful, compute, lambda current: current, running)

    running = (
        jnp.full((kv_heads, share, tok_rows), -1e30, jnp.float32),
        jnp.zeros((kv_heads, share, tok_rows), jnp.float32),
        jnp.zeros((kv_heads, share, tok_rows, head_width), jnp.float32),
    )
    own_pair = jnp.stack([key_heads, projected_value_heads])
    sink_pair = broadcast(own_pair[:, :SINKS], "seq", 0)
    running = attend(running, sink_pair, jnp.int32(0), True)
    shard_piece = lax.all_gather(own_pair, "seq", axis=1, tiled=True)
    piece_rows = shard_piece.shape[1]
    block_size = math.gcd(piece_rows, tok_rows)

    def one_slice(slice_index, inner):
        sliced = lax.dynamic_slice_in_dim(shard_piece, slice_index * block_size, block_size, 1)
        return attend(inner, sliced, slice_index * block_size, False)

    running = lax.fori_loop(0, piece_rows // block_size, one_slice, running)
    maximum, totals, weighted = running
    valid = query_pos < length_now
    result = jnp.where(valid[:, None], weighted / jnp.where(valid, totals, 1.0)[..., None], 0.0)
    return (
        result.transpose(2, 0, 1, 3).reshape(tok_rows, head_count, head_width).astype(jnp.bfloat16)
    )


def solution(mesh):
    in_specs = (
        P(("batch", "seq"), None, None),
        P(("batch", "seq"), None, None),
        P(("batch", "seq"), None, None),
        P("batch"),
    )
    out_specs = P(("batch", "seq"), None, None)
    return jax.shard_map(shards, mesh=mesh, in_specs=in_specs, out_specs=out_specs, check_vma=False)
```

profile of v0, /device:TPU:4, one launch (start us, length us, event | category | flops | bytes accessed | tf_op | source)
XLA Modules:
  0.0 382.0 jit_solution(8940974404311227422)
XLA Ops:
  6.5 4.4 %pad_maximum_fusion = bf16[2,512,4,256]{3,2,1,0:T(4,128)(2,1)} fusion(bf16[1,512,4,256]{3,2,1,0:T(4,128)(2,1)} %bitcast.72, bf16[1,512,4,256]{3,2,1,0:T(4,128)(2,1)} %bitcast.70), kind=kLoop, calls=%fused_computation.57 | loop fusion | flops 1048576 | bytes 4194304 | tf_op jit(solution)/shard_map/stack | solution.py:82
  11.7 2.0 copy.11
  14.5 24.6 %all-gather = bf16[32,4,4,256]{3,2,1,0:T(4,128)(2,1)S(1)} all-gather(bf16[2,4,4,256]{3,2,1,0:T(4,128)(2,1)S(1)} %fusion.35), channel_id=2, replica_groups=mesh['batch'=8,'seq'=16] {'seq'}, dimensions={0}, use_global_device_ids=true | all-gather | bytes 278528 | tf_op jit(solution)/shard_map/all_gather | solution.py:12
  39.1 7.7 %conditional.2 = (f32[4,2,512]{2,1,0:T(2,128)}, f32[4,2,512]{2,1,0:T(2,128)S(1)}, f32[4,2,512,256]{3,2,1,0:T(8,128)}) conditional(s32[]{:T(128)} %convert_element_type.33, () %tuple.61, (s32[512]{0:T(512)S(1)}, s32[4]{0:T(128)S(1)}, s32[]{:T(128)}, s32[4]{0:T(128)S(1)}, bf16[16,2,4,4,256]{4,3,2,1,0:T(4,128)(2,1)S(1)}, ...), branch_computations={%region_0.1_spmd, %region_1.4_spmd} | conditional | flops 17998340 | bytes 7222344 | solution.py:75
  41.9 0.8 fusion.4
  42.7 0.7 fusion.12
  43.5 3.3 convolution_add_fusion
  46.8 164.4 %all-gather.3.cloned.1.call-done = bf16[2,8192,4,256]{3,2,1,0:T(4,128)(2,1)} async-done(((bf16[2,512,4,256]{3,2,1,0:T(4,128)(2,1)}), bf16[2,8192,4,256]{3,2,1,0:T(4,128)(2,1)}) %all-gather.3.cloned.1.call-update) | async-done | bytes 33554448 | tf_op jit(solution)/shard_map/all_gather | solution.py:85
  211.2 23.1 %copy.13 = bf16[2,8192,4,256]{3,1,2,0:T(8,128)(2,1)} copy(bf16[2,8192,4,256]{3,2,1,0:T(4,128)(2,1)} %all-gather.3.cloned.1.call-done) | data formatting | bytes 67108864
  234.3 135.7 %while.22 = (s32[]{:T(128)}, f32[4,2,512]{2,1,0:T(2,128)}, f32[4,2,512]{2,1,0:T(2,128)S(1)}, f32[4,2,512,256]{3,2,1,0:T(8,128)}, s32[]{:T(128)}, /*index=5*/s32[...) while((s32[]{:T(128)}, f32[4,2,512]{2,1,0:T(2,128)}, ...), condition=%wide.region_9.10_spmd.clone, body=%wide.region_4.9_spmd.clone.sunk | while | flops 2174495232 | bytes 39079348 | solution.py:93
  234.9 13.8 %conditional.5 = ((f32[4,2,512]{2,1,0:T(2,128)}, f32[4,2,512]{2,1,0:T(2,128)S(1)}, f32[4,2,512,256]{3,2,1,0:T(8,128)})) conditional(s32[]{:T(128)} %convert_element_type.46, (f32[4,2,512]{2,1,0:T(2,128)}, f32[4,2,512]{2,1,0:T(2,128)S(1)}, f32[4,2,512,256]{3,2,1,0:T(8,128)}) %tuple.89, (s32[]{:T(128)}, s32[]{:T(128)}, s32[512]{0:T(512)S(1)}, ...), branch_computations={%region_5.5_spmd, %region_6.8_spmd} | conditional | flops 2174495232 | bytes 39076968 | solution.py:75
  236.1 2.8 fusion.13
  239.6 1.7 fusion.17
  242.0 6.2 %multiply_add_fusion = f32[4,2,512,256]{3,2,1,0:T(8,128)} fusion(f32[4,2,512,256]{3,2,1,0:T(8,128)} %get-tuple-element.461, f32[4,2,512]{2,1,0:T(2,128)S(1)} %bitcast.74, f32[4,512,512,2]{2,1,3,0:T(8,128)S(1)} %get-tuple-element.568, f32[4,2,512]{2,1,0:T(2,128)S(1)} %max.4, pred[512,512]{0,1:T(8,128)(4,1)S(1)} %fusion.30, ...), kind=kOutput, calls=%fused_computation.30 | convolution fusion | flops 1084227584 | bytes 18120712 | tf_op jit(solution)/shard_map/while/body/eval_jaxpr/cond/branch_1_fun/hgqk,khd->hgqd/dot_general | solution.py:67
  249.5 13.8 %conditional.5 = ((f32[4,2,512]{2,1,0:T(2,128)}, f32[4,2,512]{2,1,0:T(2,128)S(1)}, f32[4,2,512,256]{3,2,1,0:T(8,128)})) conditional(s32[]{:T(128)} %convert_element_type.46, (f32[4,2,512]{2,1,0:T(2,128)}, f32[4,2,512]{2,1,0:T(2,128)S(1)}, f32[4,2,512,256]{3,2,1,0:T(8,128)}) %tuple.89, (s32[]{:T(128)}, s32[]{:T(128)}, s32[512]{0:T(512)S(1)}, ...), branch_computations={%region_5.5_spmd, %region_6.8_spmd} | conditional | flops 2174495232 | bytes 39076968 | solution.py:75
  250.6 2.7 fusion.13
  254.1 1.7 fusion.17
  256.5 6.2 %multiply_add_fusion = f32[4,2,512,256]{3,2,1,0:T(8,128)} fusion(f32[4,2,512,256]{3,2,1,0:T(8,128)} %get-tuple-element.461, f32[4,2,512]{2,1,0:T(2,128)S(1)} %bitcast.74, f32[4,512,512,2]{2,1,3,0:T(8,128)S(1)} %get-tuple-element.568, f32[4,2,512]{2,1,0:T(2,128)S(1)} %max.4, pred[512,512]{0,1:T(8,128)(4,1)S(1)} %fusion.30, ...), kind=kOutput, calls=%fused_computation.30 | convolution fusion | flops 1084227584 | bytes 18120712 | tf_op jit(solution)/shard_map/while/body/eval_jaxpr/cond/branch_1_fun/hgqk,khd->hgqd/dot_general | solution.py:67
  264.0 13.8 %conditional.5 = ((f32[4,2,512]{2,1,0:T(2,128)}, f32[4,2,512]{2,1,0:T(2,128)S(1)}, f32[4,2,512,256]{3,2,1,0:T(8,128)})) conditional(s32[]{:T(128)} %convert_element_type.46, (f32[4,2,512]{2,1,0:T(2,128)}, f32[4,2,512]{2,1,0:T(2,128)S(1)}, f32[4,2,512,256]{3,2,1,0:T(8,128)}) %tuple.89, (s32[]{:T(128)}, s32[]{:T(128)}, s32[512]{0:T(512)S(1)}, ...), branch_computations={%region_5.5_spmd, %region_6.8_spmd} | conditional | flops 2174495232 | bytes 39076968 | solution.py:75
  265.1 2.8 fusion.13
  268.6 1.7 fusion.17
  271.1 6.2 %multiply_add_fusion = f32[4,2,512,256]{3,2,1,0:T(8,128)} fusion(f32[4,2,512,256]{3,2,1,0:T(8,128)} %get-tuple-element.461, f32[4,2,512]{2,1,0:T(2,128)S(1)} %bitcast.74, f32[4,512,512,2]{2,1,3,0:T(8,128)S(1)} %get-tuple-element.568, f32[4,2,512]{2,1,0:T(2,128)S(1)} %max.4, pred[512,512]{0,1:T(8,128)(4,1)S(1)} %fusion.30, ...), kind=kOutput, calls=%fused_computation.30 | convolution fusion | flops 1084227584 | bytes 18120712 | tf_op jit(solution)/shard_map/while/body/eval_jaxpr/cond/branch_1_fun/hgqk,khd->hgqd/dot_general | solution.py:67
  278.5 13.8 %conditional.5 = ((f32[4,2,512]{2,1,0:T(2,128)}, f32[4,2,512]{2,1,0:T(2,128)S(1)}, f32[4,2,512,256]{3,2,1,0:T(8,128)})) conditional(s32[]{:T(128)} %convert_element_type.46, (f32[4,2,512]{2,1,0:T(2,128)}, f32[4,2,512]{2,1,0:T(2,128)S(1)}, f32[4,2,512,256]{3,2,1,0:T(8,128)}) %tuple.89, (s32[]{:T(128)}, s32[]{:T(128)}, s32[512]{0:T(512)S(1)}, ...), branch_computations={%region_5.5_spmd, %region_6.8_spmd} | conditional | flops 2174495232 | bytes 39076968 | solution.py:75
  279.6 2.8 fusion.13
  283.1 1.7 fusion.17
  285.6 6.2 %multiply_add_fusion = f32[4,2,512,256]{3,2,1,0:T(8,128)} fusion(f32[4,2,512,256]{3,2,1,0:T(8,128)} %get-tuple-element.461, f32[4,2,512]{2,1,0:T(2,128)S(1)} %bitcast.74, f32[4,512,512,2]{2,1,3,0:T(8,128)S(1)} %get-tuple-element.568, f32[4,2,512]{2,1,0:T(2,128)S(1)} %max.4, pred[512,512]{0,1:T(8,128)(4,1)S(1)} %fusion.30, ...), kind=kOutput, calls=%fused_computation.30 | convolution fusion | flops 1084227584 | bytes 18120712 | tf_op jit(solution)/shard_map/while/body/eval_jaxpr/cond/branch_1_fun/hgqk,khd->hgqd/dot_general | solution.py:67
  293.0 13.8 %conditional.5 = ((f32[4,2,512]{2,1,0:T(2,128)}, f32[4,2,512]{2,1,0:T(2,128)S(1)}, f32[4,2,512,256]{3,2,1,0:T(8,128)})) conditional(s32[]{:T(128)} %convert_element_type.46, (f32[4,2,512]{2,1,0:T(2,128)}, f32[4,2,512]{2,1,0:T(2,128)S(1)}, f32[4,2,512,256]{3,2,1,0:T(8,128)}) %tuple.89, (s32[]{:T(128)}, s32[]{:T(128)}, s32[512]{0:T(512)S(1)}, ...), branch_computations={%region_5.5_spmd, %region_6.8_spmd} | conditional | flops 2174495232 | bytes 39076968 | solution.py:75
  294.1 2.8 fusion.13
  297.6 1.7 fusion.17
  300.1 6.2 %multiply_add_fusion = f32[4,2,512,256]{3,2,1,0:T(8,128)} fusion(f32[4,2,512,256]{3,2,1,0:T(8,128)} %get-tuple-element.461, f32[4,2,512]{2,1,0:T(2,128)S(1)} %bitcast.74, f32[4,512,512,2]{2,1,3,0:T(8,128)S(1)} %get-tuple-element.568, f32[4,2,512]{2,1,0:T(2,128)S(1)} %max.4, pred[512,512]{0,1:T(8,128)(4,1)S(1)} %fusion.30, ...), kind=kOutput, calls=%fused_computation.30 | convolution fusion | flops 1084227584 | bytes 18120712 | tf_op jit(solution)/shard_map/while/body/eval_jaxpr/cond/branch_1_fun/hgqk,khd->hgqd/dot_general | solution.py:67
  307.5 13.8 %conditional.5 = ((f32[4,2,512]{2,1,0:T(2,128)}, f32[4,2,512]{2,1,0:T(2,128)S(1)}, f32[4,2,512,256]{3,2,1,0:T(8,128)})) conditional(s32[]{:T(128)} %convert_element_type.46, (f32[4,2,512]{2,1,0:T(2,128)}, f32[4,2,512]{2,1,0:T(2,128)S(1)}, f32[4,2,512,256]{3,2,1,0:T(8,128)}) %tuple.89, (s32[]{:T(128)}, s32[]{:T(128)}, s32[512]{0:T(512)S(1)}, ...), branch_computations={%region_5.5_spmd, %region_6.8_spmd} | conditional | flops 2174495232 | bytes 39076968 | solution.py:75
  308.7 2.8 fusion.13
  312.2 1.7 fusion.17
  314.6 6.2 %multiply_add_fusion = f32[4,2,512,256]{3,2,1,0:T(8,128)} fusion(f32[4,2,512,256]{3,2,1,0:T(8,128)} %get-tuple-element.461, f32[4,2,512]{2,1,0:T(2,128)S(1)} %bitcast.74, f32[4,512,512,2]{2,1,3,0:T(8,128)S(1)} %get-tuple-element.568, f32[4,2,512]{2,1,0:T(2,128)S(1)} %max.4, pred[512,512]{0,1:T(8,128)(4,1)S(1)} %fusion.30, ...), kind=kOutput, calls=%fused_computation.30 | convolution fusion | flops 1084227584 | bytes 18120712 | tf_op jit(solution)/shard_map/while/body/eval_jaxpr/cond/branch_1_fun/hgqk,khd->hgqd/dot_general | solution.py:67
  322.0 13.8 %conditional.5 = ((f32[4,2,512]{2,1,0:T(2,128)}, f32[4,2,512]{2,1,0:T(2,128)S(1)}, f32[4,2,512,256]{3,2,1,0:T(8,128)})) conditional(s32[]{:T(128)} %convert_element_type.46, (f32[4,2,512]{2,1,0:T(2,128)}, f32[4,2,512]{2,1,0:T(2,128)S(1)}, f32[4,2,512,256]{3,2,1,0:T(8,128)}) %tuple.89, (s32[]{:T(128)}, s32[]{:T(128)}, s32[512]{0:T(512)S(1)}, ...), branch_computations={%region_5.5_spmd, %region_6.8_spmd} | conditional | flops 2174495232 | bytes 39076968 | solution.py:75
  323.2 2.8 fusion.13
  326.7 1.7 fusion.17
  329.1 6.2 %multiply_add_fusion = f32[4,2,512,256]{3,2,1,0:T(8,128)} fusion(f32[4,2,512,256]{3,2,1,0:T(8,128)} %get-tuple-element.461, f32[4,2,512]{2,1,0:T(2,128)S(1)} %bitcast.74, f32[4,512,512,2]{2,1,3,0:T(8,128)S(1)} %get-tuple-element.568, f32[4,2,512]{2,1,0:T(2,128)S(1)} %max.4, pred[512,512]{0,1:T(8,128)(4,1)S(1)} %fusion.30, ...), kind=kOutput, calls=%fused_computation.30 | convolution fusion | flops 1084227584 | bytes 18120712 | tf_op jit(solution)/shard_map/while/body/eval_jaxpr/cond/branch_1_fun/hgqk,khd->hgqd/dot_general | solution.py:67
  336.6 13.8 %conditional.5 = ((f32[4,2,512]{2,1,0:T(2,128)}, f32[4,2,512]{2,1,0:T(2,128)S(1)}, f32[4,2,512,256]{3,2,1,0:T(8,128)})) conditional(s32[]{:T(128)} %convert_element_type.46, (f32[4,2,512]{2,1,0:T(2,128)}, f32[4,2,512]{2,1,0:T(2,128)S(1)}, f32[4,2,512,256]{3,2,1,0:T(8,128)}) %tuple.89, (s32[]{:T(128)}, s32[]{:T(128)}, s32[512]{0:T(512)S(1)}, ...), branch_computations={%region_5.5_spmd, %region_6.8_spmd} | conditional | flops 2174495232 | bytes 39076968 | solution.py:75
  337.7 2.8 fusion.13
  341.2 1.7 fusion.17
  343.7 6.2 %multiply_add_fusion = f32[4,2,512,256]{3,2,1,0:T(8,128)} fusion(f32[4,2,512,256]{3,2,1,0:T(8,128)} %get-tuple-element.461, f32[4,2,512]{2,1,0:T(2,128)S(1)} %bitcast.74, f32[4,512,512,2]{2,1,3,0:T(8,128)S(1)} %get-tuple-element.568, f32[4,2,512]{2,1,0:T(2,128)S(1)} %max.4, pred[512,512]{0,1:T(8,128)(4,1)S(1)} %fusion.30, ...), kind=kOutput, calls=%fused_computation.30 | convolution fusion | flops 1084227584 | bytes 18120712 | tf_op jit(solution)/shard_map/while/body/eval_jaxpr/cond/branch_1_fun/hgqk,khd->hgqd/dot_general | solution.py:67
  351.1 13.8 %conditional.5 = ((f32[4,2,512]{2,1,0:T(2,128)}, f32[4,2,512]{2,1,0:T(2,128)S(1)}, f32[4,2,512,256]{3,2,1,0:T(8,128)})) conditional(s32[]{:T(128)} %convert_element_type.46, (f32[4,2,512]{2,1,0:T(2,128)}, f32[4,2,512]{2,1,0:T(2,128)S(1)}, f32[4,2,512,256]{3,2,1,0:T(8,128)}) %tuple.89, (s32[]{:T(128)}, s32[]{:T(128)}, s32[512]{0:T(512)S(1)}, ...), branch_computations={%region_5.5_spmd, %region_6.8_spmd} | conditional | flops 2174495232 | bytes 39076968 | solution.py:75
  352.2 2.8 fusion.13
  355.7 1.7 fusion.17
  358.2 6.2 %multiply_add_fusion = f32[4,2,512,256]{3,2,1,0:T(8,128)} fusion(f32[4,2,512,256]{3,2,1,0:T(8,128)} %get-tuple-element.461, f32[4,2,512]{2,1,0:T(2,128)S(1)} %bitcast.74, f32[4,512,512,2]{2,1,3,0:T(8,128)S(1)} %get-tuple-element.568, f32[4,2,512]{2,1,0:T(2,128)S(1)} %max.4, pred[512,512]{0,1:T(8,128)(4,1)S(1)} %fusion.30, ...), kind=kOutput, calls=%fused_computation.30 | convolution fusion | flops 1084227584 | bytes 18120712 | tf_op jit(solution)/shard_map/while/body/eval_jaxpr/cond/branch_1_fun/hgqk,khd->hgqd/dot_general | solution.py:67
  370.0 2.6 select_convert_fusion
  372.6 2.5 copy.20
  (92 shorter events, 32.0 us)
Async XLA Ops:
  6.5 204.7 %all-gather.3.cloned.1.call-start = ((), (), s32[]{:S(2)}) async-start(), calls=%async_computation | async-start | bytes 35651584 | tf_op jit(solution)/shard_map/all_gather | solution.py:85
  11.0 2.8 copy-start
Sparse Core Ops, SparseCore 0:
  11.1 200.0 all-gather.2
where the time goes:
time: 384 us; the launch traced here: 382 us
  waiting for transfers between devices  164 us (43%)
  matrix products  84.2 us (22%)
  other arithmetic  49.8 us (13%)
  local copies, waits for them, and re-layouts  33.1 us (9%)
  blocking collectives  24.6 us (6%)
  between operations  14.2 us (4%)
  loops' own time  11.7 us (3%)
    all_gather x1, waiting for transfers between devices, shards(): shard_piece = lax.all_gather(own_pair, 'seq', axis=1, tiled=True)  164 us
    dot_general x10, matrix products, compute(): jnp.einsum('hgqk,khd->hgqd', weights.astype(jnp.bfloat16), kv_block[1], p...  58.7 us
    dot_general x10, matrix products, compute(): jnp.einsum('qhgd,khd->hgqk', grouped, kv_block[0], preferred_element_type...  25.5 us
    unnamed x4, local copies, waits for them, and re-layouts  25.1 us
    all_gather x1, blocking collectives, broadcast(): lax.all_gather(x, axis)  24.6 us
    reduce_sum x10, other arithmetic, compute(): totals = totals * rescale + jnp.sum(weights, axis=-1)  16.4 us
    another operation x1, loops' own time, shards(): running = lax.fori_loop(0, piece_rows // block_size, one_slice, running)  10.9 us
  transfers between devices with their start and end apart: 1, of which 1 were waited for; matrix products, arithmetic and copies ran while one was open for 3% of the time, Pallas kernels for 0%

commit v1 on v0

--- a/solution.py
+++ b/solution.py
@@ -82,7 +82,15 @@
     own_pair = jnp.stack([key_heads, projected_value_heads])
     sink_pair = broadcast(own_pair[:, :SINKS], "seq", 0)
     running = attend(running, sink_pair, jnp.int32(0), True)
-    shard_piece = lax.all_gather(own_pair, "seq", axis=1, tiled=True)
+    shard_piece = jnp.concatenate(
+        jax.lax.all_to_all(
+            jnp.stack(jax.lax.psum(1, axis_name="seq") * [own_pair]),
+            "seq",
+            split_axis=0,
+            concat_axis=0,
+        ),
+        axis=1,
+    )
     piece_rows = shard_piece.shape[1]
     block_size = math.gcd(piece_rows, tok_rows)
 

time: 384 us -> 871 us (2.27)
  blocking collectives: 24.6 us -> 634 us
  waiting for transfers between devices: 164 us -> 0.01 us
  matrix products: 84.2 us -> 114 us
  local copies, waits for them, and re-layouts: 33.1 us -> 50.5 us
  between operations: 14.2 us -> 0.75 us
    all_gather x1, blocking collectives: 24.6 us -> 634 us  [broadcast(): lax.all_gather(x, axis)]
    all_gather x1 -> x0, waiting for transfers between devices: 164 us -> none  [shards(): shard_piece = lax.all_gather(own_pair, 'seq', axis=1, tiled=True)]
    dot_general x10, matrix products: 58.7 us -> 88.3 us  [compute(): jnp.einsum('hgqk,khd->hgqd', weights.astype(jnp.bfloat16), kv_block[1], p...]
    unnamed x4 -> x3, local copies, waits for them, and re-layouts: 25.1 us -> 2.11 us
    all_to_all x0 -> x1, local copies, waits for them, and re-layouts: none -> 22.9 us  [shards(): jax.lax.all_to_all(jnp.stack(jax.lax.psum(1, axis_name='seq') * [own_pair...]
    another operation x1 -> x3, local copies, waits for them, and re-layouts: 0.12 us -> 11.4 us  [the longest x1 11 us: shards(): jnp.stack(jax.lax.psum(1, axis_name='seq') * [own_pair])]
  transfers between devices with their start and end apart: 1 -> 1, of which waited for: 1 -> 0; matrix products, arithmetic and copies ran while one was open for 3% -> 1% of each run, Pallas kernels for 0% -> 0%
where the time goes in v1:
time: 871 us; the launch traced here: 867 us
  blocking collectives  634 us (73%)
  matrix products  114 us (13%)
  local copies, waits for them, and re-layouts  50.5 us (6%)
  other arithmetic  48.9 us (6%)
  loops' own time  11.9 us (1%)
    all_gather x1, blocking collectives, broadcast(): lax.all_gather(x, axis)  634 us
    dot_general x10, matrix products, compute(): jnp.einsum('hgqk,khd->hgqd', weights.astype(jnp.bfloat16), kv_block[1], p...  88.3 us
    dot_general x10, matrix products, compute(): jnp.einsum('qhgd,khd->hgqk', grouped, kv_block[0], preferred_element_type...  25.4 us
    all_to_all x1, local copies, waits for them, and re-layouts, shards(): jax.lax.all_to_all(jnp.stack(jax.lax.psum(1, axis_name='seq') * [own_pair...  22.9 us
  transfers between devices with their start and end apart: 1, of which 0 were waited for; matrix products, arithmetic and copies ran while one was open for 1% of the time, Pallas kernels for 0%

profile of v1, /device:TPU:4, one launch (start us, length us, event | category | flops | bytes accessed | tf_op | source)
XLA Modules:
  0.0 867.1 jit_solution(4571570694009640507)
XLA Ops:
  0.0 3.1 pad_maximum_fusion
  3.4 11.0 %stack.11 = bf16[16,2,512,4,256]{4,2,3,1,0:T(8,128)(2,1)} broadcast(bf16[2,512,4,256]{3,1,2,0:T(8,128)(2,1)S(1)} %copy.18), dimensions={1,2,3,4} | broadcast | bytes 35651584 | tf_op jit(solution)/shard_map/stack | solution.py:87
  14.4 7.5 all-to-all-start
  21.9 2.1 copy.16
  25.4 633.8 %all-gather = bf16[32,4,4,256]{3,2,1,0:T(4,128)(2,1)S(1)} all-gather(bf16[2,4,4,256]{3,2,1,0:T(4,128)(2,1)S(1)} %fusion.35), channel_id=2, replica_groups=mesh['batch'=8,'seq'=16] {'seq'}, dimensions={0}, use_global_device_ids=true | all-gather | bytes 278528 | tf_op jit(solution)/shard_map/all_gather | solution.py:12
  659.2 7.8 conditional.2
  662.0 3.2 convolution_add_fusion
  665.2 0.8 fusion.4
  666.9 22.9 %copy.19 = bf16[16,2,512,4,256]{4,2,0,3,1:T(8,128)(2,1)} copy(bf16[16,2,512,4,256]{4,2,3,1,0:T(8,128)(2,1)} %all-to-all-done) | data formatting | bytes 67108864 | tf_op jit(solution)/shard_map/all_to_all | solution.py:86
  689.8 172.1 %while.22 = (s32[]{:T(128)}, f32[4,2,512]{2,1,0:T(2,128)}, f32[4,2,512]{2,1,0:T(2,128)S(1)}, f32[4,2,512,256]{3,2,1,0:T(8,128)}, s32[]{:T(128)}, /*index=5*/s32[...) while((s32[]{:T(128)}, f32[4,2,512]{2,1,0:T(2,128)}, ...), condition=%wide.region_9.10_spmd.clone, body=%wide.region_4.9_spmd.clone.sunk | while | flops 2174495232 | bytes 72633808 | solution.py:101
  690.5 17.9 %conditional.5 = ((f32[4,2,512]{2,1,0:T(2,128)}, f32[4,2,512]{2,1,0:T(2,128)S(1)}, f32[4,2,512,256]{3,2,1,0:T(8,128)})) conditional(s32[]{:T(128)} %convert_element_type.46, (f32[4,2,512]{2,1,0:T(2,128)}, f32[4,2,512]{2,1,0:T(2,128)S(1)}, f32[4,2,512,256]{3,2,1,0:T(8,128)}) %tuple.89, (s32[]{:T(128)}, s32[]{:T(128)}, s32[512]{0:T(512)S(1)}, ...), branch_computations={%region_5.5_spmd, %region_6.8_spmd} | conditional | flops 2174495232 | bytes 72631424 | solution.py:75
  691.6 2.8 fusion.13
  695.1 1.8 fusion.17
  698.3 9.5 %multiply_add_fusion = f32[4,2,512,256]{3,2,1,0:T(8,128)} fusion(f32[4,2,512,256]{3,2,1,0:T(8,128)} %get-tuple-element.461, f32[4,2,512]{2,1,0:T(2,128)S(1)} %bitcast.78, f32[4,512,512,2]{2,1,3,0:T(8,128)} %copy-done, f32[4,2,512]{2,1,0:T(2,128)S(1)} %max.4, pred[512,512]{0,1:T(8,128)(4,1)S(1)} %fusion.30, ...), kind=kOutput, calls=%fused_computation.30 | convolution fusion | flops 1084227584 | bytes 18120712 | tf_op jit(solution)/shard_map/while/body/eval_jaxpr/cond/branch_1_fun/hgqk,khd->hgqd/dot_general | solution.py:67
  709.1 17.9 %conditional.5 = ((f32[4,2,512]{2,1,0:T(2,128)}, f32[4,2,512]{2,1,0:T(2,128)S(1)}, f32[4,2,512,256]{3,2,1,0:T(8,128)})) conditional(s32[]{:T(128)} %convert_element_type.46, (f32[4,2,512]{2,1,0:T(2,128)}, f32[4,2,512]{2,1,0:T(2,128)S(1)}, f32[4,2,512,256]{3,2,1,0:T(8,128)}) %tuple.89, (s32[]{:T(128)}, s32[]{:T(128)}, s32[512]{0:T(512)S(1)}, ...), branch_computations={%region_5.5_spmd, %region_6.8_spmd} | conditional | flops 2174495232 | bytes 72631424 | solution.py:75
  710.2 2.7 fusion.13
  713.7 1.8 fusion.17
  716.9 9.5 %multiply_add_fusion = f32[4,2,512,256]{3,2,1,0:T(8,128)} fusion(f32[4,2,512,256]{3,2,1,0:T(8,128)} %get-tuple-element.461, f32[4,2,512]{2,1,0:T(2,128)S(1)} %bitcast.78, f32[4,512,512,2]{2,1,3,0:T(8,128)} %copy-done, f32[4,2,512]{2,1,0:T(2,128)S(1)} %max.4, pred[512,512]{0,1:T(8,128)(4,1)S(1)} %fusion.30, ...), kind=kOutput, calls=%fused_computation.30 | convolution fusion | flops 1084227584 | bytes 18120712 | tf_op jit(solution)/shard_map/while/body/eval_jaxpr/cond/branch_1_fun/hgqk,khd->hgqd/dot_general | solution.py:67
  727.6 17.9 %conditional.5 = ((f32[4,2,512]{2,1,0:T(2,128)}, f32[4,2,512]{2,1,0:T(2,128)S(1)}, f32[4,2,512,256]{3,2,1,0:T(8,128)})) conditional(s32[]{:T(128)} %convert_element_type.46, (f32[4,2,512]{2,1,0:T(2,128)}, f32[4,2,512]{2,1,0:T(2,128)S(1)}, f32[4,2,512,256]{3,2,1,0:T(8,128)}) %tuple.89, (s32[]{:T(128)}, s32[]{:T(128)}, s32[512]{0:T(512)S(1)}, ...), branch_computations={%region_5.5_spmd, %region_6.8_spmd} | conditional | flops 2174495232 | bytes 72631424 | solution.py:75
  728.7 2.7 fusion.13
  732.3 1.8 fusion.17
  735.4 9.5 %multiply_add_fusion = f32[4,2,512,256]{3,2,1,0:T(8,128)} fusion(f32[4,2,512,256]{3,2,1,0:T(8,128)} %get-tuple-element.461, f32[4,2,512]{2,1,0:T(2,128)S(1)} %bitcast.78, f32[4,512,512,2]{2,1,3,0:T(8,128)} %copy-done, f32[4,2,512]{2,1,0:T(2,128)S(1)} %max.4, pred[512,512]{0,1:T(8,128)(4,1)S(1)} %fusion.30, ...), kind=kOutput, calls=%fused_computation.30 | convolution fusion | flops 1084227584 | bytes 18120712 | tf_op jit(solution)/shard_map/while/body/eval_jaxpr/cond/branch_1_fun/hgqk,khd->hgqd/dot_general | solution.py:67
  746.2 17.9 %conditional.5 = ((f32[4,2,512]{2,1,0:T(2,128)}, f32[4,2,512]{2,1,0:T(2,128)S(1)}, f32[4,2,512,256]{3,2,1,0:T(8,128)})) conditional(s32[]{:T(128)} %convert_element_type.46, (f32[4,2,512]{2,1,0:T(2,128)}, f32[4,2,512]{2,1,0:T(2,128)S(1)}, f32[4,2,512,256]{3,2,1,0:T(8,128)}) %tuple.89, (s32[]{:T(128)}, s32[]{:T(128)}, s32[512]{0:T(512)S(1)}, ...), branch_computations={%region_5.5_spmd, %region_6.8_spmd} | conditional | flops 2174495232 | bytes 72631424 | solution.py:75
  747.3 2.7 fusion.13
  750.8 1.8 fusion.17
  754.0 9.5 %multiply_add_fusion = f32[4,2,512,256]{3,2,1,0:T(8,128)} fusion(f32[4,2,512,256]{3,2,1,0:T(8,128)} %get-tuple-element.461, f32[4,2,512]{2,1,0:T(2,128)S(1)} %bitcast.78, f32[4,512,512,2]{2,1,3,0:T(8,128)} %copy-done, f32[4,2,512]{2,1,0:T(2,128)S(1)} %max.4, pred[512,512]{0,1:T(8,128)(4,1)S(1)} %fusion.30, ...), kind=kOutput, calls=%fused_computation.30 | convolution fusion | flops 1084227584 | bytes 18120712 | tf_op jit(solution)/shard_map/while/body/eval_jaxpr/cond/branch_1_fun/hgqk,khd->hgqd/dot_general | solution.py:67
  764.7 17.9 %conditional.5 = ((f32[4,2,512]{2,1,0:T(2,128)}, f32[4,2,512]{2,1,0:T(2,128)S(1)}, f32[4,2,512,256]{3,2,1,0:T(8,128)})) conditional(s32[]{:T(128)} %convert_element_type.46, (f32[4,2,512]{2,1,0:T(2,128)}, f32[4,2,512]{2,1,0:T(2,128)S(1)}, f32[4,2,512,256]{3,2,1,0:T(8,128)}) %tuple.89, (s32[]{:T(128)}, s32[]{:T(128)}, s32[512]{0:T(512)S(1)}, ...), branch_computations={%region_5.5_spmd, %region_6.8_spmd} | conditional | flops 2174495232 | bytes 72631424 | solution.py:75
  765.9 2.8 fusion.13
  769.4 1.8 fusion.17
  772.5 9.5 %multiply_add_fusion = f32[4,2,512,256]{3,2,1,0:T(8,128)} fusion(f32[4,2,512,256]{3,2,1,0:T(8,128)} %get-tuple-element.461, f32[4,2,512]{2,1,0:T(2,128)S(1)} %bitcast.78, f32[4,512,512,2]{2,1,3,0:T(8,128)} %copy-done, f32[4,2,512]{2,1,0:T(2,128)S(1)} %max.4, pred[512,512]{0,1:T(8,128)(4,1)S(1)} %fusion.30, ...), kind=kOutput, calls=%fused_computation.30 | convolution fusion | flops 1084227584 | bytes 18120712 | tf_op jit(solution)/shard_map/while/body/eval_jaxpr/cond/branch_1_fun/hgqk,khd->hgqd/dot_general | solution.py:67
  783.3 17.9 %conditional.5 = ((f32[4,2,512]{2,1,0:T(2,128)}, f32[4,2,512]{2,1,0:T(2,128)S(1)}, f32[4,2,512,256]{3,2,1,0:T(8,128)})) conditional(s32[]{:T(128)} %convert_element_type.46, (f32[4,2,512]{2,1,0:T(2,128)}, f32[4,2,512]{2,1,0:T(2,128)S(1)}, f32[4,2,512,256]{3,2,1,0:T(8,128)}) %tuple.89, (s32[]{:T(128)}, s32[]{:T(128)}, s32[512]{0:T(512)S(1)}, ...), branch_computations={%region_5.5_spmd, %region_6.8_spmd} | conditional | flops 2174495232 | bytes 72631424 | solution.py:75
  784.4 2.8 fusion.13
  787.9 1.8 fusion.17
  791.1 9.5 %multiply_add_fusion = f32[4,2,512,256]{3,2,1,0:T(8,128)} fusion(f32[4,2,512,256]{3,2,1,0:T(8,128)} %get-tuple-element.461, f32[4,2,512]{2,1,0:T(2,128)S(1)} %bitcast.78, f32[4,512,512,2]{2,1,3,0:T(8,128)} %copy-done, f32[4,2,512]{2,1,0:T(2,128)S(1)} %max.4, pred[512,512]{0,1:T(8,128)(4,1)S(1)} %fusion.30, ...), kind=kOutput, calls=%fused_computation.30 | convolution fusion | flops 1084227584 | bytes 18120712 | tf_op jit(solution)/shard_map/while/body/eval_jaxpr/cond/branch_1_fun/hgqk,khd->hgqd/dot_general | solution.py:67
  801.8 17.9 %conditional.5 = ((f32[4,2,512]{2,1,0:T(2,128)}, f32[4,2,512]{2,1,0:T(2,128)S(1)}, f32[4,2,512,256]{3,2,1,0:T(8,128)})) conditional(s32[]{:T(128)} %convert_element_type.46, (f32[4,2,512]{2,1,0:T(2,128)}, f32[4,2,512]{2,1,0:T(2,128)S(1)}, f32[4,2,512,256]{3,2,1,0:T(8,128)}) %tuple.89, (s32[]{:T(128)}, s32[]{:T(128)}, s32[512]{0:T(512)S(1)}, ...), branch_computations={%region_5.5_spmd, %region_6.8_spmd} | conditional | flops 2174495232 | bytes 72631424 | solution.py:75
  803.0 2.8 fusion.13
  806.5 1.8 fusion.17
  809.7 9.5 %multiply_add_fusion = f32[4,2,512,256]{3,2,1,0:T(8,128)} fusion(f32[4,2,512,256]{3,2,1,0:T(8,128)} %get-tuple-element.461, f32[4,2,512]{2,1,0:T(2,128)S(1)} %bitcast.78, f32[4,512,512,2]{2,1,3,0:T(8,128)} %copy-done, f32[4,2,512]{2,1,0:T(2,128)S(1)} %max.4, pred[512,512]{0,1:T(8,128)(4,1)S(1)} %fusion.30, ...), kind=kOutput, calls=%fused_computation.30 | convolution fusion | flops 1084227584 | bytes 18120712 | tf_op jit(solution)/shard_map/while/body/eval_jaxpr/cond/branch_1_fun/hgqk,khd->hgqd/dot_general | solution.py:67
  820.4 17.9 %conditional.5 = ((f32[4,2,512]{2,1,0:T(2,128)}, f32[4,2,512]{2,1,0:T(2,128)S(1)}, f32[4,2,512,256]{3,2,1,0:T(8,128)})) conditional(s32[]{:T(128)} %convert_element_type.46, (f32[4,2,512]{2,1,0:T(2,128)}, f32[4,2,512]{2,1,0:T(2,128)S(1)}, f32[4,2,512,256]{3,2,1,0:T(8,128)}) %tuple.89, (s32[]{:T(128)}, s32[]{:T(128)}, s32[512]{0:T(512)S(1)}, ...), branch_computations={%region_5.5_spmd, %region_6.8_spmd} | conditional | flops 2174495232 | bytes 72631424 | solution.py:75
  821.5 2.8 fusion.13
  825.1 1.8 fusion.17
  828.2 9.5 %multiply_add_fusion = f32[4,2,512,256]{3,2,1,0:T(8,128)} fusion(f32[4,2,512,256]{3,2,1,0:T(8,128)} %get-tuple-element.461, f32[4,2,512]{2,1,0:T(2,128)S(1)} %bitcast.78, f32[4,512,512,2]{2,1,3,0:T(8,128)} %copy-done, f32[4,2,512]{2,1,0:T(2,128)S(1)} %max.4, pred[512,512]{0,1:T(8,128)(4,1)S(1)} %fusion.30, ...), kind=kOutput, calls=%fused_computation.30 | convolution fusion | flops 1084227584 | bytes 18120712 | tf_op jit(solution)/shard_map/while/body/eval_jaxpr/cond/branch_1_fun/hgqk,khd->hgqd/dot_general | solution.py:67
  839.0 17.9 %conditional.5 = ((f32[4,2,512]{2,1,0:T(2,128)}, f32[4,2,512]{2,1,0:T(2,128)S(1)}, f32[4,2,512,256]{3,2,1,0:T(8,128)})) conditional(s32[]{:T(128)} %convert_element_type.46, (f32[4,2,512]{2,1,0:T(2,128)}, f32[4,2,512]{2,1,0:T(2,128)S(1)}, f32[4,2,512,256]{3,2,1,0:T(8,128)}) %tuple.89, (s32[]{:T(128)}, s32[]{:T(128)}, s32[512]{0:T(512)S(1)}, ...), branch_computations={%region_5.5_spmd, %region_6.8_spmd} | conditional | flops 2174495232 | bytes 72631424 | solution.py:75
  840.1 2.8 fusion.13
  843.6 1.8 fusion.17
  846.8 9.5 %multiply_add_fusion = f32[4,2,512,256]{3,2,1,0:T(8,128)} fusion(f32[4,2,512,256]{3,2,1,0:T(8,128)} %get-tuple-element.461, f32[4,2,512]{2,1,0:T(2,128)S(1)} %bitcast.78, f32[4,512,512,2]{2,1,3,0:T(8,128)} %copy-done, f32[4,2,512]{2,1,0:T(2,128)S(1)} %max.4, pred[512,512]{0,1:T(8,128)(4,1)S(1)} %fusion.30, ...), kind=kOutput, calls=%fused_computation.30 | convolution fusion | flops 1084227584 | bytes 18120712 | tf_op jit(solution)/shard_map/while/body/eval_jaxpr/cond/branch_1_fun/hgqk,khd->hgqd/dot_general | solution.py:67
  861.9 2.6 select_convert_fusion
  864.6 2.5 copy.26
  (111 shorter events, 39.4 us)
Async XLA Ops:
  14.4 652.5 %all-to-all-start = ((bf16[16,2,512,4,256]{4,2,3,1,0:T(8,128)(2,1)}), bf16[16,2,512,4,256]{4,2,3,1,0:T(8,128)(2,1)}, u32[]{:S(2)}, u32[]{:S(2)}) async-start(bf16[16,2,512,4,256]{4,2,3,1,0:T(8,128)(2,1)} %stack.11), calls=%async_computation | async-start | bytes 67108864 | tf_op jit(solution)/shard_map/all_to_all | solution.py:86
  21.9 2.8 copy-start.1
  694.4 3.2 copy-start
  712.9 3.2 copy-start
  731.5 3.2 copy-start
  750.1 3.2 copy-start
  768.6 3.2 copy-start
  787.2 3.2 copy-start
  805.7 3.2 copy-start
  824.3 3.2 copy-start
  842.9 3.2 copy-start
